TPU v7x, 32 devices: a whole 2x2x4 slice. The times are simulated.
32 devices in a mesh: rep: 4 (over y, x), tp: 8 (over z, core).
Axes of the slice: x: 2, y: 2, z: 4, core: 2. Of those that a mesh axis runs over, the one named last changes fastest.
Arguments:
- residual: bfloat16 [4, 1024, 4096], P('rep', 'tp'), may hold values from -6 to 6
- gate_pre: bfloat16 [4, 1024, 7168], P('rep', None, 'tp'), may hold values from -6 to 6
- up_pre: bfloat16 [4, 1024, 7168], P('rep', None, 'tp'), may hold values from -6 to 6
- down_weight: bfloat16 [7168, 4096], P('tp'), may hold values from -0.0625 to 0.0625
- d_out: bfloat16 [4, 1024, 4096], P('rep', 'tp'), may hold values from -1.5 to 1.5
- comp_index: int32 [4, 112, 2048], P('rep', 'tp'), may hold values from 0 to 4095
- comp_value: bfloat16 [4, 112, 2048], P('rep', 'tp'), may hold values from -48 to 48
Outputs:
- output: bfloat16 [4, 1024, 4096], P('rep', 'tp')
- gate_preact_gradient: bfloat16 [4, 1024, 7168], P('rep', None, 'tp')
- up_grad: bfloat16 [4, 1024, 7168], P('rep', None, 'tp')
- weight_grad: bfloat16 [4, 7168, 4096], P('rep', 'tp')
- update: bfloat16 [7168, 4096], P('tp')
- updated_down_weight: bfloat16 [7168, 4096], P('tp')
Inputs may be any that keep to these rules, and one draw needn't show every extreme that they name: `comp_index`: positions of one list may repeat.
All inputs are finite; a program needn't handle non-finite values.
Results may differ from a plain program's by a relative error of at most 0.011.
Values may be sent and summed in bfloat16 or wider, within the bound.
A program may use at most 320 MiB of HBM per device.

v0:
```python
import jax
import jax.numpy as jnp
from jax import lax
from jax.sharding import PartitionSpec as P

SPAN = 64
TOPK = 32


learn_rate = 0.02


def cosine_table(length):
    freq = jnp.arange(length, dtype=jnp.float32)[:, None]
    place = jnp.arange(length, dtype=jnp.float32)[None, :]
    scales = jnp.where(freq == 0, jnp.sqrt(1.0 / length), jnp.sqrt(2.0 / length))
    return scales * jnp.cos(jnp.pi * (2.0 * place + 1.0) * freq / (2.0 * length))


def decode(index_rows, value_rows):
    replicas = index_rows.shape[0]
    row_count = index_rows.shape[1]
    col_count = index_rows.shape[2] // TOPK
    cosine_basis = cosine_table(SPAN)
    positions = jnp.arange(SPAN, dtype=jnp.int32)

    def span_row(operands):
        indices, amounts = operands
        indices = jnp.transpose(indices.reshape(replicas, col_count, TOPK), (1, 0, 2)).reshape(
            col_count, replicas * TOPK
        )
        amounts = jnp.transpose(amounts.reshape(replicas, col_count, TOPK), (1, 0, 2)).reshape(
            col_count, replicas * TOPK
        )
        row_hot = ((indices // SPAN)[:, :, None] == positions).astype(jnp.bfloat16) * amounts[
            :, :, None
        ]
        col_hot = ((indices % SPAN)[:, :, None] == positions).astype(jnp.bfloat16)
        spectral_coefficients = jnp.einsum(
            "ckp,ckq->cpq", row_hot, col_hot, preferred_element_type=jnp.float32
        )
        halfway_finished = jnp.einsum(
            "kxt,ta->kxa", spectral_coefficients, cosine_basis, precision=lax.Precision.HIGHEST
        )
        output_block_list = jnp.einsum(
            "nk,hnm->khm", cosine_basis, halfway_finished, precision=lax.Precision.HIGHEST
        )
        return output_block_list.reshape(SPAN, col_count * SPAN)

    decoded = lax.map(
        span_row, (jnp.transpose(index_rows, (1, 0, 2)), jnp.transpose(value_rows, (1, 0, 2)))
    )
    return (decoded.reshape(row_count * SPAN, col_count * SPAN) / replicas).astype(jnp.bfloat16)


def shards(residual, gate_pre, up_pre, down_weight, d_out, comp_index, comp_value):
    residual_r = residual[0]
    gate_r = gate_pre[0]
    up_r = up_pre[0]
    grads_r = d_out[0]
    gate_f = gate_r.astype(jnp.float32)
    up_f = up_r.astype(jnp.float32)
    sigmoid_g = jax.nn.sigmoid(gate_f)
    activated = gate_f * sigmoid_g
    hidden = (activated * up_f).astype(jnp.bfloat16)
    summed = lax.psum_scatter(
        jnp.dot(hidden, down_weight, preferred_element_type=jnp.float32).astype(jnp.bfloat16),
        "tp",
        scatter_dimension=0,
        tiled=True,
    ).astype(jnp.float32)
    incoming = lax.all_gather(grads_r, "tp", axis=0, tiled=True)
    from_out = lax.dot_general(
        incoming, down_weight, (((1,), (1,)), ((), ())), preferred_element_type=jnp.float32
    )
    hidden_grad = from_out
    weight_sum = lax.dot_general(
        hidden, incoming, (((0,), (0,)), ((), ())), preferred_element_type=jnp.float32
    )
    weight_sum, hidden_grad = (weight_sum, hidden_grad)
    output = (residual_r.astype(jnp.float32) + summed).astype(jnp.bfloat16)
    gate_preact_gradient = (
        hidden_grad * up_f * sigmoid_g * (1.0 + gate_f * (1.0 - sigmoid_g))
    ).astype(jnp.bfloat16)
    up_grad = (hidden_grad * activated).astype(jnp.bfloat16)
    index_all, value_all = (
        lax.all_gather(comp_index, "rep", axis=0, tiled=True),
        lax.all_gather(comp_value, "rep", axis=0, tiled=True),
    )
    update = decode(index_all, value_all)
    updated_down_weight = (
        down_weight.astype(jnp.float32) - learn_rate * update.astype(jnp.float32)
    ).astype(jnp.bfloat16)
    return (
        output[None],
        gate_preact_gradient[None],
        up_grad[None],
        weight_sum.astype(jnp.bfloat16)[None],
        update,
        updated_down_weight,
    )


def solution(mesh):
    return jax.shard_map(
        shards,
        mesh=mesh,
        in_specs=(
            P("rep", "tp", None),
            P("rep", None, "tp"),
            P("rep", None, "tp"),
            P("tp", None),
            P("rep", "tp", None),
            P("rep", "tp", None),
            P("rep", "tp", None),
        ),
        out_specs=(
            P("rep", "tp", None),
            P("rep", None, "tp"),
            P("rep", None, "tp"),
            P("rep", "tp", None),
            P("tp", None),
            P("tp", None),
        ),
        check_vma=False,
    )
```

profile of v0, /device:TPU:0, one launch (start us, length us, event | category | flops | bytes accessed | tf_op | source)
XLA Modules:
  0.0 281.2 jit_solution(584213634740163432)
XLA Ops:
  7.9 14.8 %convolution_convert_fusion = bf16[1024,4096]{1,0:T(8,128)(2,1)} fusion(bf16[896,4096]{1,0:T(8,128)(2,1)} %param.12, bf16[1,1024,896]{2,1,0:T(8,128)(2,1)} %param.11, bf16[1,1024,896]{2,1,0:T(8,128)(2,1)} %param.10), kind=kOutput, calls=%fused_computation.43 | convolution fusion | flops 7527727104 | bytes 19398656 | tf_op jit(solution)/shard_map/dot_general | solution.py:67
  23.6 11.3 %all_gather.10 = s32[4,14,2048]{2,1,0:T(8,128)S(1)} all-gather(s32[1,14,2048]{2,1,0:T(8,128)S(1)} %copy.28), channel_id=1, replica_groups=mesh['rep'=4,'tp'=8] {'rep'}, dimensions={0}, use_global_device_ids=true | all-gather | bytes 573440 | tf_op jit(solution)/shard_map/all_gather | solution.py:87
  35.0 9.5 %all_gather.11 = bf16[4,14,2048]{2,1,0:T(8,128)(2,1)S(1)} all-gather(bf16[1,14,2048]{2,1,0:T(8,128)(2,1)S(1)} %copy-done.2), channel_id=1, replica_groups=mesh['rep'=4,'tp'=8] {'rep'}, dimensions={0}, use_global_device_ids=true | all-gather | bytes 286720 | tf_op jit(solution)/shard_map/all_gather | solution.py:88
  44.7 156.4 %while.14 = (s32[]{:T(128)}, f32[14,64,4096]{1,2,0:T(8,128)}, s32[14,4,2048]{2,0,1:T(8,128)S(1)}, bf16[14,4,2048]{2,1,0:T(4,128)(2,1)S(1)}, f32[64]{0:T(128)S(1)}, /*index=5*/f32[64]{0:T(128)S(1)}, s32[]{:T(128)}) while((s32[]{:T(128)}, f32[14,64,4096]{1,2,0:T(8,128)}, s32[14,4,2048]{2,0,1:T(8,128)S(1)}, ...), condition=%wide.region_2.3_spmd.clone.clone, body=%wide.region_1.2_spmd.clone.clone.sunk | while | flops 471515136 | bytes 9094741 | solution.py:50
  46.2 6.2 %fusion.67 = f32[64,64,64]{1,2,0:T(8,128)S(1)} fusion(f32[64,64,64]{2,1,0:T(8,128)S(1)} %fusion.66, f32[64]{0:T(128)S(1)} %get-tuple-element.212, f32[64]{0:T(128)S(1)} %get-tuple-element.213), kind=kOutput, calls=%fused_computation.22.clone.1 | convolution fusion | flops 201338880 | bytes 2097664 | tf_op jit(solution)/shard_map/while/body/eval_jaxpr/kxt,ta->kxa/dot_general | solution.py:42
  52.4 2.0 fusion.68
  54.4 1.5 constant_dynamic-update-slice_fusion.2
  57.4 6.2 %fusion.67 = f32[64,64,64]{1,2,0:T(8,128)S(1)} fusion(f32[64,64,64]{2,1,0:T(8,128)S(1)} %fusion.66, f32[64]{0:T(128)S(1)} %get-tuple-element.212, f32[64]{0:T(128)S(1)} %get-tuple-element.213), kind=kOutput, calls=%fused_computation.22.clone.1 | convolution fusion | flops 201338880 | bytes 2097664 | tf_op jit(solution)/shard_map/while/body/eval_jaxpr/kxt,ta->kxa/dot_general | solution.py:42
  63.6 2.0 fusion.68
  68.5 6.2 %fusion.67 = f32[64,64,64]{1,2,0:T(8,128)S(1)} fusion(f32[64,64,64]{2,1,0:T(8,128)S(1)} %fusion.66, f32[64]{0:T(128)S(1)} %get-tuple-element.212, f32[64]{0:T(128)S(1)} %get-tuple-element.213), kind=kOutput, calls=%fused_computation.22.clone.1 | convolution fusion | flops 201338880 | bytes 2097664 | tf_op jit(solution)/shard_map/while/body/eval_jaxpr/kxt,ta->kxa/dot_general | solution.py:42
  74.7 2.0 fusion.68
  76.7 1.5 constant_dynamic-update-slice_fusion.2
  79.7 6.2 %fusion.67 = f32[64,64,64]{1,2,0:T(8,128)S(1)} fusion(f32[64,64,64]{2,1,0:T(8,128)S(1)} %fusion.66, f32[64]{0:T(128)S(1)} %get-tuple-element.212, f32[64]{0:T(128)S(1)} %get-tuple-element.213), kind=kOutput, calls=%fused_computation.22.clone.1 | convolution fusion | flops 201338880 | bytes 2097664 | tf_op jit(solution)/shard_map/while/body/eval_jaxpr/kxt,ta->kxa/dot_general | solution.py:42
  85.9 2.0 fusion.68
  87.9 1.5 constant_dynamic-update-slice_fusion.2
  90.9 6.2 %fusion.67 = f32[64,64,64]{1,2,0:T(8,128)S(1)} fusion(f32[64,64,64]{2,1,0:T(8,128)S(1)} %fusion.66, f32[64]{0:T(128)S(1)} %get-tuple-element.212, f32[64]{0:T(128)S(1)} %get-tuple-element.213), kind=kOutput, calls=%fused_computation.22.clone.1 | convolution fusion | flops 201338880 | bytes 2097664 | tf_op jit(solution)/shard_map/while/body/eval_jaxpr/kxt,ta->kxa/dot_general | solution.py:42
  97.1 2.0 fusion.68
  99.1 1.5 constant_dynamic-update-slice_fusion.2
  102.1 6.2 %fusion.67 = f32[64,64,64]{1,2,0:T(8,128)S(1)} fusion(f32[64,64,64]{2,1,0:T(8,128)S(1)} %fusion.66, f32[64]{0:T(128)S(1)} %get-tuple-element.212, f32[64]{0:T(128)S(1)} %get-tuple-element.213), kind=kOutput, calls=%fused_computation.22.clone.1 | convolution fusion | flops 201338880 | bytes 2097664 | tf_op jit(solution)/shard_map/while/body/eval_jaxpr/kxt,ta->kxa/dot_general | solution.py:42
  108.3 2.0 fusion.68
  110.3 1.5 constant_dynamic-update-slice_fusion.2
  113.3 6.2 %fusion.67 = f32[64,64,64]{1,2,0:T(8,128)S(1)} fusion(f32[64,64,64]{2,1,0:T(8,128)S(1)} %fusion.66, f32[64]{0:T(128)S(1)} %get-tuple-element.212, f32[64]{0:T(128)S(1)} %get-tuple-element.213), kind=kOutput, calls=%fused_computation.22.clone.1 | convolution fusion | flops 201338880 | bytes 2097664 | tf_op jit(solution)/shard_map/while/body/eval_jaxpr/kxt,ta->kxa/dot_general | solution.py:42
  119.5 2.0 fusion.68
  121.5 1.5 constant_dynamic-update-slice_fusion.2
  124.4 6.2 %fusion.67 = f32[64,64,64]{1,2,0:T(8,128)S(1)} fusion(f32[64,64,64]{2,1,0:T(8,128)S(1)} %fusion.66, f32[64]{0:T(128)S(1)} %get-tuple-element.212, f32[64]{0:T(128)S(1)} %get-tuple-element.213), kind=kOutput, calls=%fused_computation.22.clone.1 | convolution fusion | flops 201338880 | bytes 2097664 | tf_op jit(solution)/shard_map/while/body/eval_jaxpr/kxt,ta->kxa/dot_general | solution.py:42
  130.6 2.0 fusion.68
  135.6 6.2 %fusion.67 = f32[64,64,64]{1,2,0:T(8,128)S(1)} fusion(f32[64,64,64]{2,1,0:T(8,128)S(1)} %fusion.66, f32[64]{0:T(128)S(1)} %get-tuple-element.212, f32[64]{0:T(128)S(1)} %get-tuple-element.213), kind=kOutput, calls=%fused_computation.22.clone.1 | convolution fusion | flops 201338880 | bytes 2097664 | tf_op jit(solution)/shard_map/while/body/eval_jaxpr/kxt,ta->kxa/dot_general | solution.py:42
  141.8 2.0 fusion.68
  146.8 6.2 %fusion.67 = f32[64,64,64]{1,2,0:T(8,128)S(1)} fusion(f32[64,64,64]{2,1,0:T(8,128)S(1)} %fusion.66, f32[64]{0:T(128)S(1)} %get-tuple-element.212, f32[64]{0:T(128)S(1)} %get-tuple-element.213), kind=kOutput, calls=%fused_computation.22.clone.1 | convolution fusion | flops 201338880 | bytes 2097664 | tf_op jit(solution)/shard_map/while/body/eval_jaxpr/kxt,ta->kxa/dot_general | solution.py:42
  152.9 2.0 fusion.68
  157.9 6.2 %fusion.67 = f32[64,64,64]{1,2,0:T(8,128)S(1)} fusion(f32[64,64,64]{2,1,0:T(8,128)S(1)} %fusion.66, f32[64]{0:T(128)S(1)} %get-tuple-element.212, f32[64]{0:T(128)S(1)} %get-tuple-element.213), kind=kOutput, calls=%fused_computation.22.clone.1 | convolution fusion | flops 201338880 | bytes 2097664 | tf_op jit(solution)/shard_map/while/body/eval_jaxpr/kxt,ta->kxa/dot_general | solution.py:42
  164.1 2.0 fusion.68
  166.1 1.5 constant_dynamic-update-slice_fusion.2
  169.1 6.2 %fusion.67 = f32[64,64,64]{1,2,0:T(8,128)S(1)} fusion(f32[64,64,64]{2,1,0:T(8,128)S(1)} %fusion.66, f32[64]{0:T(128)S(1)} %get-tuple-element.212, f32[64]{0:T(128)S(1)} %get-tuple-element.213), kind=kOutput, calls=%fused_computation.22.clone.1 | convolution fusion | flops 201338880 | bytes 2097664 | tf_op jit(solution)/shard_map/while/body/eval_jaxpr/kxt,ta->kxa/dot_general | solution.py:42
  175.3 2.0 fusion.68
  177.3 1.5 constant_dynamic-update-slice_fusion.2
  180.3 6.2 %fusion.67 = f32[64,64,64]{1,2,0:T(8,128)S(1)} fusion(f32[64,64,64]{2,1,0:T(8,128)S(1)} %fusion.66, f32[64]{0:T(128)S(1)} %get-tuple-element.212, f32[64]{0:T(128)S(1)} %get-tuple-element.213), kind=kOutput, calls=%fused_computation.22.clone.1 | convolution fusion | flops 201338880 | bytes 2097664 | tf_op jit(solution)/shard_map/while/body/eval_jaxpr/kxt,ta->kxa/dot_general | solution.py:42
  186.5 2.0 fusion.68
  188.5 1.5 constant_dynamic-update-slice_fusion.2
  191.5 6.2 %fusion.67 = f32[64,64,64]{1,2,0:T(8,128)S(1)} fusion(f32[64,64,64]{2,1,0:T(8,128)S(1)} %fusion.66, f32[64]{0:T(128)S(1)} %get-tuple-element.212, f32[64]{0:T(128)S(1)} %get-tuple-element.213), kind=kOutput, calls=%fused_computation.22.clone.1 | convolution fusion | flops 201338880 | bytes 2097664 | tf_op jit(solution)/shard_map/while/body/eval_jaxpr/kxt,ta->kxa/dot_general | solution.py:42
  197.7 2.0 fusion.68
  199.7 1.5 constant_dynamic-update-slice_fusion.2
  201.2 16.7 %multiply_convert_fusion = bf16[14,64,4096]{1,2,0:T(8,128)(2,1)} fusion(f32[14,64,4096]{1,2,0:T(8,128)} %get-tuple-element.92), kind=kLoop, calls=%fused_computation.37 | loop fusion | flops 7340032 | bytes 22020096 | tf_op jit(solution)/shard_map/convert_element_type | solution.py:53
  217.8 14.0 %copy.31 = bf16[14,64,4096]{2,1,0:T(8,128)(2,1)} copy(bf16[14,64,4096]{1,2,0:T(8,128)(2,1)} %multiply_convert_fusion) | data formatting | bytes 14680064 | tf_op jit(solution)/shard_map/convert_element_type | solution.py:53
  231.8 12.4 %subtract_convert_fusion = bf16[896,4096]{1,0:T(8,128)(2,1)} fusion(bf16[896,4096]{1,0:T(8,128)(2,1)} %param.12, bf16[14,64,4096]{2,1,0:T(8,128)(2,1)} %copy.31), kind=kLoop, calls=%fused_computation.38 | loop fusion | flops 18350080 | bytes 22020096 | tf_op jit(solution)/shard_map/convert_element_type | solution.py:93
  244.2 13.5 %convert_bitcast_fusion = bf16[1,896,4096]{2,1,0:T(8,128)(2,1)} fusion(bf16[1,1024,4096]{2,1,0:T(8,128)(2,1)} %all-gather.3.cloned.1.call-done, bf16[1,1024,896]{2,1,0:T(8,128)(2,1)S(1)} %copy-done.4, bf16[1,1024,896]{2,1,0:T(8,128)(2,1)} %param.10), kind=kOutput, calls=%fused_computation.44 | convolution fusion | flops 7527202816 | bytes 19398656 | tf_op jit(solution)/shard_map/dot_general | solution.py:77
  257.8 14.1 %fusion.42 = (bf16[1,1024,896]{2,1,0:T(8,128)(2,1)}, bf16[1,1024,896]{2,1,0:T(8,128)(2,1)}) fusion(bf16[1,1024,896]{2,1,0:T(8,128)(2,1)S(1)} %copy-done.5, bf16[1,1024,896]{2,1,0:T(8,128)(2,1)S(1)} %copy-done.4, bf16[896,4096]{1,0:T(8,128)(2,1)} %param.12, bf16[1,1024,4096]{2,1,0:T(8,128)(2,1)S(1)} %copy-done.3), kind=kOutput, calls=%fused_computation.61 | convolution fusion | flops 7529955328 | bytes 23068672 | tf_op jit(solution)/shard_map/dot_general | solution.py:73
  271.9 2.4 fusion.44
  (194 shorter events, 27.8 us)
Async XLA Ops:
  7.2 237.0 %all-gather.3.cloned.1.call-start = ((), (), s32[]{:S(2)}) async-start(), calls=%async_computation.2 | async-start | bytes 9437184 | tf_op jit(solution)/shard_map/all_gather | solution.py:72
  7.9 264.0 %reduce-scatter.2.cloned.1.call-start = ((), (), s32[]{:S(2)}) async-start(), calls=%async_computation.1 | async-start | bytes 9437184 | tf_op jit(solution)/shard_map/reduce_scatter | solution.py:66
  22.7 0.9 copy-start.1
  22.7 12.3 %copy-start.2 = (bf16[1,14,2048]{2,1,0:T(8,128)(2,1)S(1)}, bf16[1,14,2048]{2,1,0:T(8,128)(2,1)}, u32[]{:S(2)}) copy-start(bf16[1,14,2048]{2,1,0:T(8,128)(2,1)} %param.15) | copy-start | bytes 172036
  231.8 12.4 %copy-start.4 = (bf16[1,1024,896]{2,1,0:T(8,128)(2,1)S(1)}, bf16[1,1024,896]{2,1,0:T(8,128)(2,1)}, u32[]{:S(2)}) copy-start(bf16[1,1024,896]{2,1,0:T(8,128)(2,1)} %param.11) | copy-start | bytes 5505028
  244.2 13.5 %copy-start.3 = (bf16[1,1024,4096]{2,1,0:T(8,128)(2,1)S(1)}, bf16[1,1024,4096]{2,1,0:T(8,128)(2,1)}, u32[]{:S(2)}) copy-start(bf16[1,1024,4096]{2,1,0:T(8,128)(2,1)} %all-gather.3.cloned.1.call-done) | copy-start | bytes 25165828
  244.2 13.5 %copy-start.5 = (bf16[1,1024,896]{2,1,0:T(8,128)(2,1)S(1)}, bf16[1,1024,896]{2,1,0:T(8,128)(2,1)}, u32[]{:S(2)}) copy-start(bf16[1,1024,896]{2,1,0:T(8,128)(2,1)} %param.10) | copy-start | bytes 5505028
  257.7 14.2 %copy-start = (bf16[1,128,4096]{2,1,0:T(8,128)(2,1)S(1)}, bf16[1,128,4096]{2,1,0:T(8,128)(2,1)}, u32[]{:S(2)}) copy-start(bf16[1,128,4096]{2,1,0:T(8,128)(2,1)} %param.9) | copy-start | bytes 3145732
Sparse Core Ops, SparseCore 0:
  9.6 84.7 all-gather.2
  96.7 88.0 reduce-scatter.1
where the time goes:
time: 282 us; the launch traced here: 281 us
  matrix products  167 us (59%)
  local copies, waits for them, and re-layouts  45.2 us (16%)
  other arithmetic  32.4 us (11%)
  blocking collectives  20.9 us (7%)
  between operations  14.1 us (5%)
    dot_general x14, matrix products, span_row(): jnp.einsum('kxt,ta->kxa', spectral_coefficients, cosine_basis, precision=...  86.7 us
    dot_general x14, matrix products, span_row(): jnp.einsum('nk,hnm->khm', cosine_basis, halfway_finished, precision=lax.P...  28.1 us
    dynamic_update_slice x14, local copies, waits for them, and re-layouts, decode(): lax.map(span_row, (jnp.transpose(index_rows, (1, 0, 2)), jnp.transpose(va...  20.6 us
    convert_element_type x1, other arithmetic, decode(): (decoded.reshape(row_count * SPAN, col_count * SPAN) / replicas).astype(j...  16.7 us
    dot_general x1, matrix products, shards(): jnp.dot(hidden, down_weight, preferred_element_type=jnp.float32)  14.8 us
    dot_general x1, matrix products, shards(): lax.dot_general(incoming, down_weight, (((1,), (1,)), ((), ())), preferre...  14.1 us
    convert_element_type x1, local copies, waits for them, and re-layouts, decode(): (decoded.reshape(row_count * SPAN, col_count * SPAN) / replicas).astype(j...  14 us
    dot_general x1, matrix products, shards(): lax.dot_general(hidden, incoming, (((0,), (0,)), ((), ())), preferred_ele...  13.5 us
  transfers between devices with their start and end apart: 2, of which 0 were waited for; matrix products, arithmetic and copies ran while one was open for 86% of the time, Pallas kernels for 0%

commit v1 on v0

v1 whole, which is shorter than its diff:
```python
import functools

import jax
import jax.numpy as jnp
import numpy as np
from jax import lax
from jax.experimental import pallas as pl
from jax.experimental.pallas import tpu as pltpu
from jax.sharding import PartitionSpec as P

SPAN = 64
TOPK = 32


learn_rate = 0.02


LANES = 128


def cosine_table(length):
    freq = np.arange(length, dtype=np.float64)[:, None]
    place = np.arange(length, dtype=np.float64)[None, :]
    scales = np.where(freq == 0, np.sqrt(1.0 / length), np.sqrt(2.0 / length))
    return scales * np.cos(np.pi * (2.0 * place + 1.0) * freq / (2.0 * length))


def decode_kernel(count, *refs):
    index_refs, value_refs = refs[:count], refs[count:2 * count]
    weight_ref, right_ref, left_ref, update_ref, weight_out_ref, mixed_ref = refs[2 * count:]
    groups = index_refs[0].shape[1] // LANES
    per_group = LANES // TOPK
    width = per_group * SPAN
    depth = count * LANES
    lane = lax.broadcasted_iota(jnp.int32, (1, depth), 1)
    shift = ((lane // TOPK) % per_group) * SPAN
    row_place = lax.broadcasted_iota(jnp.int32, (SPAN, depth), 0).astype(jnp.float32).astype(jnp.bfloat16)
    col_place = lax.broadcasted_iota(jnp.int32, (width, depth), 0).astype(jnp.float32).astype(jnp.bfloat16)

    def gather(group, carry):
        at = pl.ds(pl.multiple_of(group * LANES, LANES), LANES)
        words = jnp.concatenate([ref[:, at] for ref in index_refs], axis=1)
        values = jnp.concatenate([ref[:, at] for ref in value_refs], axis=1).astype(jnp.bfloat16)
        rows = (words >> (SPAN.bit_length() - 1)).astype(jnp.float32).astype(jnp.bfloat16)
        cols = ((words & (SPAN - 1)) + shift).astype(jnp.float32).astype(jnp.bfloat16)
        row_hot = jnp.where(rows == row_place, values, jnp.bfloat16(0))
        col_hot = jnp.where(cols == col_place, jnp.bfloat16(1), jnp.bfloat16(0))
        spectral = lax.dot_general(
            row_hot, col_hot, (((1,), (1,)), ((), ())), preferred_element_type=jnp.float32
        )
        mixed_ref[pl.ds(pl.multiple_of(group * SPAN, SPAN), SPAN), :] = spectral.astype(jnp.bfloat16)
        return carry

    lax.fori_loop(0, groups, gather, 0, unroll=UNROLL)
    halfway = jnp.dot(
        mixed_ref[...], right_ref[...], preferred_element_type=jnp.float32
    ).astype(jnp.bfloat16)
    for group in range(groups):
        block = jnp.dot(
            left_ref[...], halfway[group * SPAN:(group + 1) * SPAN], preferred_element_type=jnp.float32
        )
        change = (block * (1.0 / count)).astype(jnp.bfloat16)
        at = slice(group * width, (group + 1) * width)
        update_ref[:, at] = change
        weight_out_ref[:, at] = (
            weight_ref[:, at].astype(jnp.float32) - learn_rate * change.astype(jnp.float32)
        ).astype(jnp.bfloat16)


UNROLL = 4


def decode(indices, values, down_weight):
    count = len(indices)
    span_rows, _, listed = indices[0].shape
    units, model = down_weight.shape
    basis = cosine_table(SPAN)
    per_group = LANES // TOPK
    width = per_group * SPAN
    right = jnp.asarray(np.kron(np.eye(per_group), basis), jnp.bfloat16)
    left = jnp.asarray(basis.T, jnp.bfloat16)
    strip = pl.BlockSpec((SPAN, model), lambda a: (a, 0))
    whole = lambda shape: pl.BlockSpec(shape, lambda a: (0, 0))
    return pl.pallas_call(
        functools.partial(decode_kernel, count),
        grid=(span_rows,),
        out_shape=[jax.ShapeDtypeStruct((units, model), jnp.bfloat16)] * 2,
        in_specs=[pl.BlockSpec((None, 1, listed), lambda a: (a, 0, 0))] * (2 * count)
        + [strip, whole((width, width)), whole((SPAN, SPAN))],
        out_specs=[strip, strip],
        scratch_shapes=[pltpu.VMEM((listed // LANES * SPAN, width), jnp.bfloat16)],
        compiler_params=pltpu.CompilerParams(
            dimension_semantics=("arbitrary",), vmem_limit_bytes=24 * 2**20
        ),
        cost_estimate=pl.CostEstimate(
            flops=20 * 10**9, bytes_accessed=units * model * 6, transcendentals=0
        ),
        name="decode",
    )(*indices, *values, down_weight, right, left)


def shards(residual, gate_pre, up_pre, down_weight, d_out, comp_index, comp_value):
    residual_r = residual[0]
    gate_r = gate_pre[0]
    up_r = up_pre[0]
    grads_r = d_out[0]
    replicas = lax.axis_size("rep")

    def from_replicas(mine):
        return [mine] + [
            lax.ppermute(mine, "rep", [(i, (i + step) % replicas) for i in range(replicas)])
            for step in range(1, replicas)
        ]

    indices = from_replicas(comp_index[0][:, None])
    values = from_replicas(comp_value[0].astype(jnp.float32)[:, None])
    gate_f = gate_r.astype(jnp.float32)
    up_f = up_r.astype(jnp.float32)
    sigmoid_g = jax.nn.sigmoid(gate_f)
    activated = gate_f * sigmoid_g
    hidden = (activated * up_f).astype(jnp.bfloat16)
    summed = lax.psum_scatter(
        jnp.dot(hidden, down_weight, preferred_element_type=jnp.float32).astype(jnp.bfloat16),
        "tp",
        scatter_dimension=0,
        tiled=True,
    ).astype(jnp.float32)
    incoming = lax.all_gather(grads_r, "tp", axis=0, tiled=True)
    from_out = lax.dot_general(
        incoming, down_weight, (((1,), (1,)), ((), ())), preferred_element_type=jnp.float32
    )
    hidden_grad = from_out
    weight_sum = lax.dot_general(
        hidden, incoming, (((0,), (0,)), ((), ())), preferred_element_type=jnp.float32
    )
    weight_sum, hidden_grad = (weight_sum, hidden_grad)
    output = (residual_r.astype(jnp.float32) + summed).astype(jnp.bfloat16)
    gate_preact_gradient = (
        hidden_grad * up_f * sigmoid_g * (1.0 + gate_f * (1.0 - sigmoid_g))
    ).astype(jnp.bfloat16)
    up_grad = (hidden_grad * activated).astype(jnp.bfloat16)
    update, updated_down_weight = decode(indices, values, down_weight)
    return (
        output[None],
        gate_preact_gradient[None],
        up_grad[None],
        weight_sum.astype(jnp.bfloat16)[None],
        update,
        updated_down_weight,
    )


def solution(mesh):
    return jax.shard_map(
        shards,
        mesh=mesh,
        in_specs=(
            P("rep", "tp", None),
            P("rep", None, "tp"),
            P("rep", None, "tp"),
            P("tp", None),
            P("rep", "tp", None),
            P("rep", "tp", None),
            P("rep", "tp", None),
        ),
        out_specs=(
            P("rep", "tp", None),
            P("rep", None, "tp"),
            P("rep", None, "tp"),
            P("rep", "tp", None),
            P("tp", None),
            P("tp", None),
        ),
        check_vma=False,
    )
```

time: 282 us -> 194 us (0.69)
  matrix products: 167 us -> 41.8 us
  waiting for transfers between devices: 0.7 us -> 87.1 us
  local copies, waits for them, and re-layouts: 45.2 us -> 3.9 us
  Pallas kernels: 0 us -> 34.5 us
  other arithmetic: 32.4 us -> 2.53 us
  blocking collectives: 20.9 us -> 0 us
  starting transfers between devices: 0.08 us -> 10 us
    dot_general x42 -> x0, matrix products: 124 us -> none  [the longest x14 86.7 us: span_row(): jnp.einsum('kxt,ta->kxa', spectral_coefficients, cosine_basis, precision=...]
    reduce_scatter x1, waiting for transfers between devices: 0.01 us -> 63.2 us  [shards(): lax.psum_scatter(jnp.dot(hidden, down_weight, preferred_element_type=jnp....]
    pallas_call x0 -> x1, Pallas kernels: none -> 34.5 us  [decode(): pl.pallas_call(functools.partial(decode_kernel, count), grid=(span_rows,)...]
    convert_element_type x2 -> x1, other arithmetic: 29.1 us -> 0.09 us  [shards(): values = from_replicas(comp_value[0].astype(jnp.float32)[:, None])]
    all_gather x2 -> x0, blocking collectives: 20.9 us -> none  [the longest x1 11.3 us: shards(): lax.all_gather(comp_index, 'rep', axis=0, tiled=True)]
    dynamic_update_slice x14 -> x0, local copies, waits for them, and re-layouts: 20.6 us -> none  [decode(): lax.map(span_row, (jnp.transpose(index_rows, (1, 0, 2)), jnp.transpose(va...]
    all_gather x1, waiting for transfers between devices: 0.01 us -> 17.1 us  [shards(): incoming = lax.all_gather(grads_r, 'tp', axis=0, tiled=True)]
    convert_element_type x1 -> x0, local copies, waits for them, and re-layouts: 14 us -> none  [decode(): (decoded.reshape(row_count * SPAN, col_count * SPAN) / replicas).astype(j...]
  transfers between devices with their start and end apart: 2 -> 8, of which waited for: 0 -> 5; matrix products, arithmetic and copies ran while one was open for 86% -> 22% of each run, Pallas kernels for 0% -> 18%
where the time goes in v1:
time: 194 us
  waiting for transfers between devices  87.1 us (45%)
  matrix products  41.8 us (22%)
  Pallas kernels  34.5 us (18%)
  between operations  14.1 us (7%)
  starting transfers between devices  10 us (5%)
  local copies, waits for them, and re-layouts  3.9 us (2%)
  other arithmetic  2.53 us (1%)
    reduce_scatter x1, waiting for transfers between devices, shards(): lax.psum_scatter(jnp.dot(hidden, down_weight, preferred_element_type=jnp....  63.2 us
    pallas_call x1, Pallas kernels, decode(): pl.pallas_call(functools.partial(decode_kernel, count), grid=(span_rows,)...  34.5 us
    all_gather x1, waiting for transfers between devices, shards(): incoming = lax.all_gather(grads_r, 'tp', axis=0, tiled=True)  17.1 us
    dot_general x1, matrix products, shards(): jnp.dot(hidden, down_weight, preferred_element_type=jnp.float32)  14.8 us
    dot_general x1, matrix products, shards(): lax.dot_general(incoming, down_weight, (((1,), (1,)), ((), ())), preferre...  13.8 us
    dot_general x1, matrix products, shards(): lax.dot_general(hidden, incoming, (((0,), (0,)), ((), ())), preferred_ele...  13.3 us
    ppermute x6, starting transfers between devices, from_replicas(): lax.ppermute(mine, 'rep', [(i, (i + step) % replicas) for i in range(repl...  9.93 us
    ppermute x6, waiting for transfers between devices, from_replicas(): lax.ppermute(mine, 'rep', [(i, (i + step) % replicas) for i in range(repl...  6.06 us
  transfers between devices with their start and end apart: 8, of which 5 were waited for; matrix products, arithmetic and copies ran while one was open for 22% of the time, Pallas kernels for 18%

profile of v1, /device:TPU:0, one launch (start us, length us, event | category | flops | bytes accessed | tf_op | source)
XLA Modules:
  0.0 194.0 jit_solution(5593333141852051729)
XLA Ops:
  7.2 0.0 all-gather.3.cloned.1.call-start
  7.2 0.7 all-gather.3.cloned.1.call-update
  7.9 0.0 reduce-scatter.2.cloned.1.call-start
  7.9 14.8 %convolution_convert_fusion = bf16[1024,4096]{1,0:T(8,128)(2,1)} fusion(bf16[896,4096]{1,0:T(8,128)(2,1)} %refs_8_.1, bf16[1,1024,896]{2,1,0:T(8,128)(2,1)} %param.11, bf16[1,1024,896]{2,1,0:T(8,128)(2,1)} %param.10), kind=kOutput, calls=%fused_computation.4 | convolution fusion | flops 7527727104 | bytes 19398656 | tf_op jit(solution)/shard_map/dot_general | solution.py:123
  22.7 0.0 copy-start.6
  22.7 0.0 copy-start.2
  22.7 0.0 copy-start.3
  22.7 0.0 copy-start.4
  22.7 0.0 copy-start.7
  22.7 0.0 reduce-scatter.2.cloned.1.call-update
  22.8 0.8 copy-done.6
  23.6 0.1 bitcast_convert_fusion.refs_4_
  23.6 4.0 %collective-permute-start.5 = (f32[14,1,2048]{2,1,0:T(1,128)S(1)}, f32[14,1,2048]{2,1,0:T(1,128)S(1)}, u32[]{:S(2)}, u32[]{:S(2)}) collective-permute-start(f32[14,1,2048]{2,1,0:T(1,128)S(1)} %bitcast_convert_fusion.refs_4_), channel_id=1, source_target_pairs={{0,24},{8,0},{16,8},{24,16},{1,25},{9,1},{17,9},{25,17},{2,26},{10... | collective-permute-start | bytes 344072 | tf_op jit(solution)/shard_map/ppermute | solution.py:111
  27.6 0.5 collective-permute-start.4
  28.1 0.5 collective-permute-start.3
  28.7 0.0 copy-done.2
  28.7 2.4 %collective-permute-start.2 = (s32[14,1,2048]{2,1,0:T(1,128)S(1)}, s32[14,1,2048]{2,1,0:T(1,128)S(1)}, u32[]{:S(2)}, u32[]{:S(2)}) collective-permute-start(s32[14,1,2048]{2,1,0:T(1,128)S(1)} %bitcast.46), channel_id=1, source_target_pairs={{0,24},{8,0},{16,8},{24,16},{1,25},{9,1},{17,9},{25,17},{2,26},{10... | collective-permute-start | bytes 344072 | tf_op jit(solution)/shard_map/ppermute | solution.py:111
  31.1 1.5 collective-permute-start.1
  32.6 0.0 collective-permute-done.5.refs_7_
  32.6 1.0 collective-permute-start
  33.6 3.4 %collective-permute-done.4.refs_6_ = f32[14,1,2048]{2,1,0:T(1,128)S(1)} collective-permute-done((f32[14,1,2048]{2,1,0:T(1,128)S(1)}, f32[14,1,2048]{2,1,0:T(1,128)S(1)}, u32[]{:S(2)}, u32[]{:S(2)}) %collective-permute-start.4) | collective-permute-done | bytes 114720 | tf_op jit(solution)/shard_map/ppermute | solution.py:111
  37.0 0.0 collective-permute-done.3.refs_5_
  37.0 0.1 collective-permute-done.2.refs_3_
  37.1 2.5 %collective-permute-done.1.refs_2_ = s32[14,1,2048]{2,1,0:T(1,128)S(1)} collective-permute-done((s32[14,1,2048]{2,1,0:T(1,128)S(1)}, s32[14,1,2048]{2,1,0:T(1,128)S(1)}, u32[]{:S(2)}, u32[]{:S(2)}) %collective-permute-start.1) | collective-permute-done | bytes 114720 | tf_op jit(solution)/shard_map/ppermute | solution.py:111
  39.6 0.0 collective-permute-done.refs_1_
  39.6 0.0 copy-done.3
  39.6 0.0 copy-done.4
  39.7 0.0 copy-start
  39.7 3.1 %copy-done = bf16[896,4096]{1,0:T(8,128)(2,1)S(1)} copy-done((bf16[896,4096]{1,0:T(8,128)(2,1)S(1)}, bf16[896,4096]{1,0:T(8,128)(2,1)}, u32[]{:S(2)}) %copy-start) | copy-done | bytes 7340056
  42.7 34.5 %decode.1 = (bf16[896,4096]{1,0:T(8,128)(2,1)}, bf16[896,4096]{1,0:T(8,128)(2,1)}) custom-call(s32[14,1,2048]{2,1,0:T(1,128)S(1)} %bitcast.49, s32[14,1,2048]{2,1,0:T(1,128)S(1)} %collective-permute-done.refs_1_, s32[14,1,2048]{2,1,0:T(1,128)S(1)} %collective-permute-done.1.refs_2_, s32[14,1,2048]{2,1,0:T(1,128)S(1)} %collective-permute-done.2.refs_3_, ...), custom_call_target="tpu_custom_call" | custom-call | flops 20000000000 | bytes 22020096 | tf_op jit(solution)/shard_map/decode/pallas_call | solution.py:84
  77.3 17.1 %all-gather.3.cloned.1.call-done = bf16[1,1024,4096]{2,1,0:T(8,128)(2,1)} async-done(((bf16[1,128,4096]{2,1,0:T(8,128)(2,1)}), bf16[1,1024,4096]{2,1,0:T(8,128)(2,1)}) %all-gather.3.cloned.1.call-update) | async-done | bytes 8388624 | tf_op jit(solution)/shard_map/all_gather | solution.py:128
  94.4 0.0 copy-done.7
  94.4 0.0 copy-start.1
  94.4 0.0 copy-start.8
  94.4 13.3 %convert_bitcast_fusion = bf16[1,896,4096]{2,1,0:T(8,128)(2,1)} fusion(bf16[1,1024,4096]{2,1,0:T(8,128)(2,1)} %all-gather.3.cloned.1.call-done, bf16[1,1024,896]{2,1,0:T(8,128)(2,1)S(1)} %copy-done.7, bf16[1,1024,896]{2,1,0:T(8,128)(2,1)} %param.10), kind=kOutput, calls=%fused_computation.5 | convolution fusion | flops 7527202816 | bytes 19398656 | tf_op jit(solution)/shard_map/dot_general | solution.py:133
  107.7 0.0 copy-done.1
  107.7 0.0 copy-done.8
  107.7 0.0 copy-start.5
  107.7 13.8 %fusion.15 = (bf16[1,1024,896]{2,1,0:T(8,128)(2,1)}, bf16[1,1024,896]{2,1,0:T(8,128)(2,1)}) fusion(bf16[1,1024,896]{2,1,0:T(8,128)(2,1)S(1)} %copy-done.8, bf16[1,1024,896]{2,1,0:T(8,128)(2,1)S(1)} %copy-done.7, bf16[896,4096]{1,0:T(8,128)(2,1)S(1)} %copy-done.1, bf16[1,1024,4096]{2,1,0:T(8,128)(2,1)} %all-gather.3.cloned.1.call-done), kind=kOutput, calls=%fused_computation.22 | convolution fusion | flops 7529955328 | bytes 23068672 | tf_op jit(solution)/shard_map/dot_general | solution.py:129
  121.5 63.2 %reduce-scatter.2.cloned.1.call-done = bf16[128,4096]{1,0:T(8,128)(2,1)} async-done(((bf16[1024,4096]{1,0:T(8,128)(2,1)}), bf16[128,4096]{1,0:T(8,128)(2,1)}) %reduce-scatter.2.cloned.1.call-update) | async-done | bytes 1048592 | tf_op jit(solution)/shard_map/reduce_scatter | solution.py:122
  184.7 0.0 copy-done.5
  184.7 2.4 %fusion.17 = bf16[1,128,4096]{2,1,0:T(8,128)(2,1)} fusion(bf16[128,4096]{1,0:T(8,128)(2,1)} %reduce-scatter.2.cloned.1.call-done, bf16[1,128,4096]{2,1,0:T(8,128)(2,1)S(1)} %copy-done.5), kind=kLoop, calls=%fused_computation.24 | loop fusion | flops 2097152 | bytes 3145728 | tf_op jit(solution)/shard_map/broadcast_in_dim | solution.py:144
Async XLA Ops:
  7.2 87.2 %all-gather.3.cloned.1.call-start = ((), (), s32[]{:S(2)}) async-start(), calls=%async_computation.2 | async-start | bytes 9437184 | tf_op jit(solution)/shard_map/all_gather | solution.py:128
  7.9 176.8 %reduce-scatter.2.cloned.1.call-start = ((), (), s32[]{:S(2)}) async-start(), calls=%async_computation.1 | async-start | bytes 9437184 | tf_op jit(solution)/shard_map/reduce_scatter | solution.py:122
  22.7 0.8 copy-start.6
  22.7 5.9 %copy-start.2 = (s32[1,14,2048]{2,0,1:T(1,128)S(1)}, s32[1,14,2048]{2,0,1:T(1,128)}, u32[]{:S(2)}) copy-start(s32[1,14,2048]{2,0,1:T(1,128)} %param.14) | copy-start | bytes 344068
  22.7 16.9 %copy-start.3 = (bf16[256,256]{1,0:T(8,128)(2,1)S(1)}, bf16[256,256]{1,0:T(8,128)(2,1)}, u32[]{:S(2)}) copy-start(bf16[256,256]{1,0:T(8,128)(2,1)} %constant.6.clone.refs_9_) | copy-start | bytes 393220
  22.7 16.9 %copy-start.4 = (bf16[64,64]{1,0:T(8,128)(2,1)S(1)}, bf16[64,64]{1,0:T(8,128)(2,1)}, u32[]{:S(2)}) copy-start(bf16[64,64]{1,0:T(8,128)(2,1)} %constant.7.clone.refs_10_) | copy-start | bytes 24580
  22.7 71.6 %copy-start.7 = (bf16[1,1024,896]{2,1,0:T(8,128)(2,1)S(1)}, bf16[1,1024,896]{2,1,0:T(8,128)(2,1)}, u32[]{:S(2)}) copy-start(bf16[1,1024,896]{2,1,0:T(8,128)(2,1)} %param.11) | copy-start | bytes 5505028
  23.6 8.9 %collective-permute-start.5 = (f32[14,1,2048]{2,1,0:T(1,128)S(1)}, f32[14,1,2048]{2,1,0:T(1,128)S(1)}, u32[]{:S(2)}, u32[]{:S(2)}) collective-permute-start(f32[14,1,2048]{2,1,0:T(1,128)S(1)} %bitcast_convert_fusion.refs_4_), channel_id=1, source_target_pairs={{0,24},{8,0},{16,8},{24,16},{1,25},{9,1},{17,9},{25,17},{2,26},{10... | collective-permute-start | bytes 344072 | tf_op jit(solution)/shard_map/ppermute | solution.py:111
  27.6 9.4 %collective-permute-start.4 = (f32[14,1,2048]{2,1,0:T(1,128)S(1)}, f32[14,1,2048]{2,1,0:T(1,128)S(1)}, u32[]{:S(2)}, u32[]{:S(2)}) collective-permute-start(f32[14,1,2048]{2,1,0:T(1,128)S(1)} %bitcast_convert_fusion.refs_4_), channel_id=1, source_target_pairs={{0,16},{8,24},{16,0},{24,8},{1,17},{9,25},{17,1},{25,9},{2,18},{10... | collective-permute-start | bytes 344072 | tf_op jit(solution)/shard_map/ppermute | solution.py:111
  28.1 8.9 %collective-permute-start.3 = (f32[14,1,2048]{2,1,0:T(1,128)S(1)}, f32[14,1,2048]{2,1,0:T(1,128)S(1)}, u32[]{:S(2)}, u32[]{:S(2)}) collective-permute-start(f32[14,1,2048]{2,1,0:T(1,128)S(1)} %bitcast_convert_fusion.refs_4_), channel_id=1, source_target_pairs={{0,8},{8,16},{16,24},{24,0},{1,9},{9,17},{17,25},{25,1},{2,10},{10... | collective-permute-start | bytes 344072 | tf_op jit(solution)/shard_map/ppermute | solution.py:111
  28.7 8.5 %collective-permute-start.2 = (s32[14,1,2048]{2,1,0:T(1,128)S(1)}, s32[14,1,2048]{2,1,0:T(1,128)S(1)}, u32[]{:S(2)}, u32[]{:S(2)}) collective-permute-start(s32[14,1,2048]{2,1,0:T(1,128)S(1)} %bitcast.46), channel_id=1, source_target_pairs={{0,24},{8,0},{16,8},{24,16},{1,25},{9,1},{17,9},{25,17},{2,26},{10... | collective-permute-start | bytes 344072 | tf_op jit(solution)/shard_map/ppermute | solution.py:111
  31.1 8.6 %collective-permute-start.1 = (s32[14,1,2048]{2,1,0:T(1,128)S(1)}, s32[14,1,2048]{2,1,0:T(1,128)S(1)}, u32[]{:S(2)}, u32[]{:S(2)}) collective-permute-start(s32[14,1,2048]{2,1,0:T(1,128)S(1)} %bitcast.47), channel_id=1, source_target_pairs={{0,16},{8,24},{16,0},{24,8},{1,17},{9,25},{17,1},{25,9},{2,18},{10... | collective-permute-start | bytes 344072 | tf_op jit(solution)/shard_map/ppermute | solution.py:111
  32.6 7.1 %collective-permute-start = (s32[14,1,2048]{2,1,0:T(1,128)S(1)}, s32[14,1,2048]{2,1,0:T(1,128)S(1)}, u32[]{:S(2)}, u32[]{:S(2)}) collective-permute-start(s32[14,1,2048]{2,1,0:T(1,128)S(1)} %bitcast.48), channel_id=1, source_target_pairs={{0,8},{8,16},{16,24},{24,0},{1,9},{9,17},{17,25},{25,1},{2,10},{10... | collective-permute-start | bytes 344072 | tf_op jit(solution)/shard_map/ppermute | solution.py:111
  39.7 3.1 %copy-start = (bf16[896,4096]{1,0:T(8,128)(2,1)S(1)}, bf16[896,4096]{1,0:T(8,128)(2,1)}, u32[]{:S(2)}) copy-start(bf16[896,4096]{1,0:T(8,128)(2,1)} %refs_8_.1) | copy-start | bytes 22020100
  94.4 13.3 %copy-start.1 = (bf16[896,4096]{1,0:T(8,128)(2,1)S(1)}, bf16[896,4096]{1,0:T(8,128)(2,1)}, u32[]{:S(2)}) copy-start(bf16[896,4096]{1,0:T(8,128)(2,1)} %refs_8_.1) | copy-start | bytes 22020100
  94.4 13.3 %copy-start.8 = (bf16[1,1024,896]{2,1,0:T(8,128)(2,1)S(1)}, bf16[1,1024,896]{2,1,0:T(8,128)(2,1)}, u32[]{:S(2)}) copy-start(bf16[1,1024,896]{2,1,0:T(8,128)(2,1)} %param.10) | copy-start | bytes 5505028
  107.7 77.0 %copy-start.5 = (bf16[1,128,4096]{2,1,0:T(8,128)(2,1)S(1)}, bf16[1,128,4096]{2,1,0:T(8,128)(2,1)}, u32[]{:S(2)}) copy-start(bf16[1,128,4096]{2,1,0:T(8,128)(2,1)} %param.9) | copy-start | bytes 3145732
Sparse Core Ops, SparseCore 0:
  9.6 84.7 all-gather.2
  96.7 88.0 reduce-scatter.1
